TPU v7x, 256 devices: a whole 4x4x8 slice. The times are simulated.
256 devices in a mesh: ctx: 64 (over z, x, core), heads: 4 (over y).
Axes of the slice: x: 4, y: 4, z: 8, core: 2. Of those that a mesh axis runs over, the one named last changes fastest.
Arguments:
- query_rows: bfloat16 [64, 16, 2, 128], P('ctx', 'heads'), may hold values from -6 to 6
- past_keys: bfloat16 [64, 16, 4096, 128], P(None, 'heads', 'ctx'), may hold values from -6 to 6
- past_values: bfloat16 [64, 16, 4096, 128], P(None, 'heads', 'ctx'), may hold values from -6 to 6
- used_length: int32 [64], replicated, may hold values from 2048 to 4096
Outputs:
- read: bfloat16 [64, 16, 2, 128], P('ctx', 'heads')
All inputs are finite; a program needn't handle non-finite values.
Results may differ from a plain program's by a relative error of at most 0.0015.
Values may be sent and summed in bfloat16 or wider, within the bound.
A program may use at most 64 MiB of HBM per device.

v0:
```python
import jax
import jax.numpy as jnp
from jax import lax
from jax.sharding import Mesh
from jax.sharding import PartitionSpec as P

HEAD_SIZE = 128
CTX = ("ctx_0", "ctx_1", "ctx_2")


def gathered_by_axis(value, axes, dim):
    for axis in reversed(axes):
        value = lax.all_gather(value, axis, axis=dim, tiled=True)
    return value


def body(query_rows, past_keys, past_values, used_length):
    all_queries = gathered_by_axis(query_rows, CTX, 0)
    logit = jnp.einsum(
        "bkgd,bktd->bkgt", all_queries, past_keys, preferred_element_type=jnp.float32
    ) * HEAD_SIZE ** (-0.5)
    positions = lax.axis_index(CTX) * past_keys.shape[2] + jnp.arange(past_keys.shape[2])
    filled = positions[None, :] < used_length[:, None]
    logit = jnp.where(filled[:, None, None, :], logit, -1e30)
    top = jnp.max(logit, axis=-1)
    part = jnp.where(filled[:, None, None, :], jnp.exp(logit - top[..., None]), 0.0)
    weight_sum = jnp.sum(part, axis=-1)
    read_sum = jnp.einsum(
        "bkgt,bktd->bkgd", part, past_values.astype(jnp.float32), precision=lax.Precision.HIGHEST
    )
    tops, sums, parts = (
        lax.all_to_all(top[None], CTX, split_axis=1, concat_axis=0, tiled=True),
        lax.all_to_all(weight_sum[None], CTX, split_axis=1, concat_axis=0, tiled=True),
        lax.all_to_all(read_sum[None], CTX, split_axis=1, concat_axis=0, tiled=True),
    )
    best = jnp.max(tops, axis=0)
    scale = jnp.exp(tops - best)
    weight_own = jnp.sum(sums * scale, axis=0)
    read_own = jnp.sum(parts * scale[..., None], axis=0)
    read = (read_own / weight_own[..., None]).astype(jnp.bfloat16)
    return read


def solution(mesh):
    finer = Mesh(
        mesh.devices.reshape(8, 4, 2, mesh.shape["heads"]), ("ctx_0", "ctx_1", "ctx_2", "heads")
    )
    return jax.shard_map(
        body,
        mesh=finer,
        in_specs=(
            P(CTX, "heads", None, None),
            P(None, "heads", CTX, None),
            P(None, "heads", CTX, None),
            P(),
        ),
        out_specs=P(CTX, "heads", None, None),
        check_vma=False,
    )
```

profile of v0, /device:TPU:1, one launch (start us, length us, event | category | flops | bytes accessed | tf_op | source)
XLA Modules:
  0.0 104.1 jit_solution(3401453398949490919)
XLA Ops:
  0.0 0.7 copy.10
  0.7 4.6 %all_gather.9 = bf16[2,4,2,128]{3,1,2,0:T(4,128)(2,1)S(1)} all-gather(bf16[1,4,2,128]{3,1,2,0:T(4,128)(2,1)S(1)} %copy.10), channel_id=1, replica_groups=mesh['ctx_0'=8,'ctx_1'=4,'ctx_2'=2,'heads'=4] {'ctx_2'}, dimensions={0}, use_global_device_ids=true | all-gather | bytes 6144 | tf_op jit(solution)/shard_map/all_gather | solution.py:13
  5.3 8.9 %all_gather.10 = bf16[8,4,2,128]{3,1,2,0:T(4,128)(2,1)S(1)} all-gather(bf16[2,4,2,128]{3,1,2,0:T(4,128)(2,1)S(1)} %all_gather.9), channel_id=1, replica_groups=mesh['ctx_0'=8,'ctx_1'=4,'ctx_2'=2,'heads'=4] {'ctx_1'}, dimensions={0}, use_global_device_ids=true | all-gather | bytes 20480 | tf_op jit(solution)/shard_map/all_gather | solution.py:13
  14.2 20.8 %all_gather.11 = bf16[64,4,2,128]{3,1,2,0:T(4,128)(2,1)S(1)} all-gather(bf16[8,4,2,128]{3,1,2,0:T(4,128)(2,1)S(1)} %all_gather.10), channel_id=1, replica_groups=mesh['ctx_0'=8,'ctx_1'=4,'ctx_2'=2,'heads'=4] {'ctx_0'}, dimensions={0}, use_global_device_ids=true | all-gather | bytes 147456 | tf_op jit(solution)/shard_map/all_gather | solution.py:13
  35.1 0.7 broadcast_compare_fusion
  35.8 4.6 %fusion.10 = (f32[64,4,2]{2,1,0:T(4,128)S(1)}, f32[64,4,2,64]{3,2,1,0:T(2,128)S(1)}) fusion(bf16[64,4,64,128]{3,2,1,0:T(8,128)(2,1)} %param.5, bf16[64,4,2,128]{3,1,2,0:T(4,128)(2,1)S(1)} %all_gather.11, pred[64,64]{1,0:T(8,128)(4,1)S(1)} %broadcast_compare_fusion), kind=kOutput, calls=%fused_computation.19 | convolution fusion | flops 8486400 | bytes 4462592 | tf_op jit(solution)/shard_map/bkgd,bktd->bkgt/dot_general | solution.py:19
  40.4 0.8 fusion.7
  41.2 1.1 %copy.15 = f32[1,64,4,2]{2,3,0,1:T(2,128)} copy(f32[1,64,4,2]{3,2,1,0:T(4,128)S(1)} %bitcast.33) | data formatting | bytes 4096 | tf_op jit(solution)/shard_map/broadcast_in_dim | solution.py:33
  42.3 16.5 %all-to-all-start.2 = ((f32[1,64,4,2]{2,3,0,1:T(2,128)}), f32[1,64,4,2]{2,3,0,1:T(2,128)S(1)}, u32[]{:S(2)}, u32[]{:S(2)}) async-start(f32[1,64,4,2]{2,3,0,1:T(2,128)} %copy.15), calls=%async_computation.2 | async-start | bytes 131072 | tf_op jit(solution)/shard_map/all_to_all | solution.py:33
  58.9 1.1 %copy.13 = f32[1,64,4,2]{2,3,0,1:T(2,128)} copy(f32[1,64,4,2]{3,2,1,0:T(4,128)S(1)} %bitcast.32) | data formatting | bytes 4096 | tf_op jit(solution)/shard_map/broadcast_in_dim | solution.py:32
  59.9 9.1 %all-to-all-done.2 = f32[1,64,4,2]{2,3,0,1:T(2,128)S(1)} async-done(((f32[1,64,4,2]{2,3,0,1:T(2,128)}), f32[1,64,4,2]{2,3,0,1:T(2,128)S(1)}, u32[]{:S(2)}, u32[]{:S(2)}) %all-to-all-start.2) | async-done | bytes 2080 | tf_op jit(solution)/shard_map/all_to_all | solution.py:33
  69.1 4.4 %all-to-all-start.1 = ((f32[1,64,4,2]{2,3,0,1:T(2,128)}), f32[1,64,4,2]{2,3,0,1:T(2,128)S(1)}, u32[]{:S(2)}, u32[]{:S(2)}) async-start(f32[1,64,4,2]{2,3,0,1:T(2,128)} %copy.13), calls=%async_computation.1 | async-start | bytes 131072 | tf_op jit(solution)/shard_map/all_to_all | solution.py:32
  73.5 5.9 %convolution_bitcast_fusion = f32[1,64,4,2,128]{4,3,2,0,1:T(2,128)} fusion(bf16[64,4,64,128]{3,2,1,0:T(8,128)(2,1)} %param.6, f32[64,4,2,64]{3,2,1,0:T(2,128)S(1)} %get-tuple-element.6, pred[64,64]{1,0:T(8,128)(4,1)S(1)} %broadcast_compare_fusion, f32[64,4,2]{2,1,0:T(4,128)S(1)} %get-tuple-element.5), kind=kOutput, calls=%fused_computation | convolution fusion | flops 50397184 | bytes 4593664 | tf_op jit(solution)/shard_map/bkgt,bktd->bkgd/dot_general | solution.py:28
  79.4 4.4 %all-to-all-done.1 = f32[1,64,4,2]{2,3,0,1:T(2,128)S(1)} async-done(((f32[1,64,4,2]{2,3,0,1:T(2,128)}), f32[1,64,4,2]{2,3,0,1:T(2,128)S(1)}, u32[]{:S(2)}, u32[]{:S(2)}) %all-to-all-start.1) | async-done | bytes 2080 | tf_op jit(solution)/shard_map/all_to_all | solution.py:32
  83.8 6.0 %all-to-all-start = ((f32[1,64,4,2,128]{4,3,2,0,1:T(2,128)}), f32[1,64,4,2,128]{4,3,2,0,1:T(2,128)S(1)}, u32[]{:S(2)}, u32[]{:S(2)}) async-start(f32[1,64,4,2,128]{4,3,2,0,1:T(2,128)} %convolution_bitcast_fusion), calls=%async_computation | async-start | bytes 524288 | tf_op jit(solution)/shard_map/all_to_all | solution.py:34
  89.8 0.1 reduce_max.19
  89.9 0.1 fusion.6
  90.0 0.1 copy.16
  90.1 0.5 copy.14
  90.6 12.5 %all-to-all-done = f32[1,64,4,2,128]{4,3,2,0,1:T(2,128)S(1)} async-done(((f32[1,64,4,2,128]{4,3,2,0,1:T(2,128)}), f32[1,64,4,2,128]{4,3,2,0,1:T(2,128)S(1)}, u32[]{:S(2)}, u32[]{:S(2)}) %all-to-all-start) | async-done | bytes 262176 | tf_op jit(solution)/shard_map/all_to_all | solution.py:34
  103.1 0.3 fusion.1
  103.5 0.7 fusion.8
  (2 shorter events, 0.0 us)
Async XLA Ops:
  42.3 26.8 %all-to-all-start.2 = ((f32[1,64,4,2]{2,3,0,1:T(2,128)}), f32[1,64,4,2]{2,3,0,1:T(2,128)S(1)}, u32[]{:S(2)}, u32[]{:S(2)}) async-start(f32[1,64,4,2]{2,3,0,1:T(2,128)} %copy.15), calls=%async_computation.2 | async-start | bytes 131072 | tf_op jit(solution)/shard_map/all_to_all | solution.py:33
  69.1 14.7 %all-to-all-start.1 = ((f32[1,64,4,2]{2,3,0,1:T(2,128)}), f32[1,64,4,2]{2,3,0,1:T(2,128)S(1)}, u32[]{:S(2)}, u32[]{:S(2)}) async-start(f32[1,64,4,2]{2,3,0,1:T(2,128)} %copy.13), calls=%async_computation.1 | async-start | bytes 131072 | tf_op jit(solution)/shard_map/all_to_all | solution.py:32
  83.8 19.4 %all-to-all-start = ((f32[1,64,4,2,128]{4,3,2,0,1:T(2,128)}), f32[1,64,4,2,128]{4,3,2,0,1:T(2,128)S(1)}, u32[]{:S(2)}, u32[]{:S(2)}) async-start(f32[1,64,4,2,128]{4,3,2,0,1:T(2,128)} %convolution_bitcast_fusion), calls=%async_computation | async-start | bytes 524288 | tf_op jit(solution)/shard_map/all_to_all | solution.py:34
where the time goes:
time: 104 us
  blocking collectives  34.4 us (33%)
  starting transfers between devices  27 us (26%)
  waiting for transfers between devices  26 us (25%)
  matrix products  10.5 us (10%)
  local copies, waits for them, and re-layouts  3.48 us (3%)
  other arithmetic  2.74 us (3%)
    all_gather x3, blocking collectives, gathered_by_axis(): value = lax.all_gather(value, axis, axis=dim, tiled=True)  34.4 us
    all_to_all x1, starting transfers between devices, body(): lax.all_to_all(weight_sum[None], CTX, split_axis=1, concat_axis=0, tiled=...  16.5 us
    all_to_all x1, waiting for transfers between devices, body(): lax.all_to_all(read_sum[None], CTX, split_axis=1, concat_axis=0, tiled=True)  12.5 us
    all_to_all x1, waiting for transfers between devices, body(): lax.all_to_all(weight_sum[None], CTX, split_axis=1, concat_axis=0, tiled=...  9.1 us
    all_to_all x1, starting transfers between devices, body(): lax.all_to_all(read_sum[None], CTX, split_axis=1, concat_axis=0, tiled=True)  6.03 us
    dot_general x1, matrix products, body(): jnp.einsum('bkgt,bktd->bkgd', part, past_values.astype(jnp.float32), prec...  5.91 us
    dot_general x1, matrix products, body(): jnp.einsum('bkgd,bktd->bkgt', all_queries, past_keys, preferred_element_t...  4.58 us
    all_to_all x1, starting transfers between devices, body(): lax.all_to_all(top[None], CTX, split_axis=1, concat_axis=0, tiled=True)  4.43 us
  transfers between devices with their start and end apart: 3, of which 3 were waited for; matrix products, arithmetic and copies ran while one was open for 8% of the time, Pallas kernels for 0%

commit v1 on v0

v1 whole, which is shorter than its diff:
```python
import functools

import jax
import jax.numpy as jnp
from jax import lax
from jax.experimental import pallas as pl
from jax.experimental.pallas import tpu as pltpu
from jax.sharding import PartitionSpec as P

HEAD_SIZE = 128
SCALE = HEAD_SIZE ** (-0.5)
NZ, NX, NC = 8, 4, 2
NW = NX * NC
NEG = -1e30
MESH = pl.DeviceIdType.MESH
F32, BF16 = jnp.float32, jnp.bfloat16


def kernel(
    q_ref, len_ref, k_ref, v_ref, o_ref,
    kbuf, vbuf, qbuf, r1s, r1r, r2s, r2r,
    ksem, vsem, q1s_sem, q1r_sem, q2s_sem, q2r_sem, r1s_sem, r1r_sem, r2s_sem, r2r_sem,
):
    me = lax.axis_index("ctx")
    z, w = me // NW, me % NW
    x, core = w // NC, w % NC

    def z_peer(dz):
        zz = lax.rem(z + dz, NZ)
        return zz, {"ctx": zz * NW + w}

    def w_at(dx, dc):
        return lax.rem(x + dx, NX) * NC + lax.rem(core + dc, NC)

    barrier = pltpu.get_barrier_semaphore()
    for dz in range(1, NZ):
        pl.semaphore_signal(barrier, inc=1, device_id=z_peer(dz)[1], device_id_type=MESH)
    for dx in range(NX):
        for dc in range(NC):
            if dx or dc:
                pl.semaphore_signal(
                    barrier, inc=1, device_id={"ctx": z * NW + w_at(dx, dc)}, device_id_type=MESH
                )

    loads = []
    for i in range(NZ):
        rows = pl.ds(i * NW, NW)
        loads.append(pltpu.make_async_copy(k_ref.at[rows], kbuf.at[rows], ksem.at[i]))
    for i in range(NZ):
        rows = pl.ds(i * NW, NW)
        loads.append(pltpu.make_async_copy(v_ref.at[rows], vbuf.at[rows], vsem.at[i]))
    for load in loads:
        load.start()
    qbuf[w, z] = q_ref[...]

    pl.semaphore_wait(barrier, NZ - 1 + NW - 1)

    sends = []

    def send(src, dst, s_sem, r_sem, ctx):
        copy = pltpu.make_async_remote_copy(
            src_ref=src, dst_ref=dst, send_sem=s_sem, recv_sem=r_sem,
            device_id={"ctx": ctx}, device_id_type=MESH,
        )
        copy.start()
        sends.append(copy)

    def arrived(ref, sem):
        pltpu.make_async_copy(ref, ref, sem).wait()

    far_z = (4, 3, 5, 2, 6, 1, 7)
    for dz in far_z:
        zz, _ = z_peer(dz)
        send(q_ref, qbuf.at[w, z], q1s_sem.at[dz], q1r_sem.at[z], zz * NW + w)
    for dz in far_z[::-1]:
        zz, _ = z_peer(dz)
        arrived(qbuf.at[w, zz], q1r_sem.at[zz])
    far_w = ((2, 0), (2, 1), (1, 0), (3, 0), (1, 1), (3, 1), (0, 1))
    for dx, dc in far_w:
        ww = w_at(dx, dc)
        send(qbuf.at[w], qbuf.at[w], q2s_sem.at[dx * NC + dc], q2r_sem.at[w], z * NW + ww)

    base = me * 64
    lane = lax.broadcasted_iota(jnp.int32, (64, 128), 1)
    row = lax.broadcasted_iota(jnp.int32, (128, 128), 0)
    row_head = (row // 2) % 4
    lane_t = lax.broadcasted_iota(jnp.int32, (8, 128), 1) % 64 + base
    lane8 = lax.broadcasted_iota(jnp.int32, (8, 128), 1)
    row2 = lax.broadcasted_iota(jnp.int32, (8, 256), 0)
    lane2 = lax.broadcasted_iota(jnp.int32, (8, 256), 1)
    own_head = (row2 // 2) == (lane2 // 64)

    for step, dx in enumerate((0, 1, 3, 2)):
        xx = lax.rem(x + dx, NX)
        if dx == 0:
            arrived(qbuf.at[w_at(0, 1)], q2r_sem.at[w_at(0, 1)])
            for load in loads[:NZ]:
                load.wait()
        else:
            for dc in range(NC):
                arrived(qbuf.at[w_at(dx, dc)], q2r_sem.at[w_at(dx, dc)])
        queries = jnp.concatenate(
            [qbuf[xx * NC + c].astype(F32).reshape(64, 128) for c in range(NC)], axis=0
        )
        weights = jnp.concatenate(
            [jnp.where(row_head == k, queries, 0.0).astype(BF16) for k in range(4)], axis=1
        )
        members = [(c, zz) for c in range(NC) for zz in range(NZ)]
        keys = jnp.concatenate(
            [
                jnp.concatenate([kbuf[zz * NW + xx * NC + c, k] for k in range(4)], axis=1)
                for c, zz in members
            ],
            axis=0,
        )
        wide = lax.dot_general(
            keys, weights, (((1,), (1,)), ((), ())), preferred_element_type=F32
        )
        logit_t = jnp.zeros((64, 128), F32)
        for i in range(len(members)):
            logit_t = jnp.where(lane // 8 == i, wide[i * 64 : (i + 1) * 64], logit_t)
        logit_all = jnp.concatenate([logit_t, logit_t], axis=0).T * SCALE
        if dx == 0:
            for load in loads[NZ:]:
                load.wait()
        stats = [jnp.zeros((8, 128), F32) for _ in range(NC)]
        for i, (c, zz) in enumerate(members):
            b = zz * NW + xx * NC + c
            filled = lane_t < len_ref[b]
            logit = jnp.where(filled, logit_all[i * 8 : (i + 1) * 8], NEG)
            top = jnp.max(logit, axis=1, keepdims=True)
            part = jnp.where(filled, jnp.exp(logit - top), 0.0)
            total = jnp.sum(part, axis=1, keepdims=True) * 0.5
            spread = jnp.where(own_head, jnp.concatenate([part, part], axis=1), 0.0)
            high = spread.astype(BF16).astype(F32)
            both = jnp.concatenate([high, spread - high], axis=0).astype(BF16)
            out = jnp.dot(both, vbuf[b].reshape(256, 128), preferred_element_type=F32)
            r1s[xx * NC + c, zz] = out[:8] + out[8:]
            stats[c] = jnp.where(lane8 == zz, top, jnp.where(lane8 == NZ + zz, total, stats[c]))
        for c in range(NC):
            r1s[xx * NC + c, NZ] = stats[c]
        if dx == 0:
            r1r[w] = r1s[w]
        for dc in range(NC):
            if dx or dc:
                ww = w_at(dx, dc)
                send(r1s.at[ww], r1r.at[w], r1s_sem.at[dx * NC + dc], r1r_sem.at[w], z * NW + ww)

    for dx, dc in far_w:
        ww = w_at(dx, dc)
        arrived(r1r.at[ww], r1r_sem.at[ww])
    st = [r1r[s, NZ] for s in range(NW)]
    best = functools.reduce(jnp.maximum, st)
    scales = [jnp.exp(t - best) for t in st]
    totals = sum(pltpu.roll(scales[s], NZ, 1) * st[s] for s in range(NW))
    for dz in far_z + (0,):
        zz = lax.rem(z + dz, NZ)
        pick = lane8 == zz
        acc = jnp.zeros((8, 128), F32)
        for s in range(NW):
            scale = jnp.sum(jnp.where(pick, scales[s], 0.0), axis=1, keepdims=True)
            acc += scale * r1r[s, zz]
        top = jnp.sum(jnp.where(pick, best, 0.0), axis=1, keepdims=True)
        total = jnp.sum(jnp.where(lane8 == NZ + zz, totals, 0.0), axis=1, keepdims=True)
        tail = jnp.where(lane8 < 64, top, total)
        if dz == 0:
            r2r[z, 0] = acc
            r2r[z, 1] = tail
        else:
            r2s[dz, 0] = acc
            r2s[dz, 1] = tail
            send(r2s.at[dz], r2r.at[z], r2s_sem.at[dz], r2r_sem.at[z], zz * NW + w)
    for dz in far_z[::-1]:
        zz = lax.rem(z + dz, NZ)
        arrived(r2r.at[zz], r2r_sem.at[zz])
    tops = [r2r[s, 1] for s in range(NZ)]
    best = functools.reduce(jnp.maximum, tops)
    acc = jnp.zeros((8, 128), F32)
    total = jnp.zeros((8, 1), F32)
    for s in range(NZ):
        scale = jnp.exp(tops[s][:, :1] - best[:, :1])
        acc += scale * r2r[s, 0]
        total += scale * tops[s][:, 64:65]
    o_ref[...] = (acc / total).astype(o_ref.dtype)
    for copy in sends:
        copy.wait_send()


def body(query_rows, past_keys, past_values, used_length):
    vmem, dma = pltpu.VMEM, pltpu.SemaphoreType.DMA
    out = pl.pallas_call(
        kernel,
        out_shape=jax.ShapeDtypeStruct((8, HEAD_SIZE), BF16),
        in_specs=[
            pl.BlockSpec(memory_space=pltpu.VMEM),
            pl.BlockSpec(memory_space=pltpu.SMEM),
            pl.BlockSpec(memory_space=pl.ANY),
            pl.BlockSpec(memory_space=pl.ANY),
        ],
        out_specs=pl.BlockSpec(memory_space=pltpu.VMEM),
        scratch_shapes=[
            vmem(past_keys.shape, BF16),
            vmem(past_values.shape, BF16),
            vmem((NW, NZ, 8, HEAD_SIZE), BF16),
            vmem((NW, NZ + 1, 8, HEAD_SIZE), F32),
            vmem((NW, NZ + 1, 8, HEAD_SIZE), F32),
            vmem((NZ, 2, 8, HEAD_SIZE), F32),
            vmem((NZ, 2, 8, HEAD_SIZE), F32),
            dma((NZ,)), dma((NZ,)),
            dma((NZ,)), dma((NZ,)), dma((NW,)), dma((NW,)),
            dma((NW,)), dma((NW,)), dma((NZ,)), dma((NZ,)),
        ],
        compiler_params=pltpu.CompilerParams(collective_id=0, has_side_effects=True),
    )(query_rows.reshape(8, HEAD_SIZE), used_length, past_keys, past_values)
    return out.reshape(query_rows.shape)


def solution(mesh):
    return jax.shard_map(
        body,
        mesh=mesh,
        in_specs=(
            P("ctx", "heads", None, None),
            P(None, "heads", "ctx", None),
            P(None, "heads", "ctx", None),
            P(),
        ),
        out_specs=P("ctx", "heads", None, None),
        check_vma=False,
    )
```

time: 104 us -> 33.2 us (0.32)
  blocking collectives: 34.4 us -> 0 us
  Pallas kernels: 0 us -> 31.7 us
  starting transfers between devices: 27 us -> 0 us
  waiting for transfers between devices: 26 us -> 0 us
  matrix products: 10.5 us -> 0 us
  other arithmetic: 2.74 us -> 0 us
  local copies, waits for them, and re-layouts: 3.48 us -> 1.26 us
    all_gather x3 -> x0, blocking collectives: 34.4 us -> none  [gathered_by_axis(): value = lax.all_gather(value, axis, axis=dim, tiled=True)]
    pallas_call x0 -> x1, Pallas kernels: none -> 31.7 us  [body(): pl.pallas_call(kernel, out_shape=jax.ShapeDtypeStruct((8, HEAD_SIZE), BF1...]
    all_to_all x3 -> x0, starting transfers between devices: 27 us -> none  [the longest x1 16.5 us: body(): lax.all_to_all(weight_sum[None], CTX, split_axis=1, concat_axis=0, tiled=...]
    all_to_all x3 -> x0, waiting for transfers between devices: 26 us -> none  [the longest x1 12.5 us: body(): lax.all_to_all(read_sum[None], CTX, split_axis=1, concat_axis=0, tiled=True)]
    dot_general x2 -> x0, matrix products: 10.5 us -> none  [the longest x1 5.91 us: body(): jnp.einsum('bkgt,bktd->bkgd', part, past_values.astype(jnp.float32), prec...]
    broadcast_in_dim x2 -> x0, local copies, waits for them, and re-layouts: 2.2 us -> none  [the longest x1 1.1 us: body(): weight_sum[None]]
    reduce_sum x3 -> x0, other arithmetic: 1.22 us -> none  [the longest x1 0.78 us: body(): weight_sum = jnp.sum(part, axis=-1)]
  transfers between devices with their start and end apart: 3 -> 0, of which waited for: 3 -> 0; matrix products, arithmetic and copies ran while one was open for 8% -> 0% of each run, Pallas kernels for 0% -> 0%
where the time goes in v1:
time: 33.2 us; the launch traced here: 33 us
  Pallas kernels  31.7 us (95%)
  local copies, waits for them, and re-layouts  1.26 us (4%)
    pallas_call x1, Pallas kernels, body(): pl.pallas_call(kernel, out_shape=jax.ShapeDtypeStruct((8, HEAD_SIZE), BF1...  31.7 us
    unnamed x1, local copies, waits for them, and re-layouts  1.26 us

profile of v1, /device:TPU:1, one launch (start us, length us, event | category | flops | bytes accessed | tf_op | source)
XLA Modules:
  0.0 33.0 jit_solution(1831102046087043456)
XLA Ops:
  0.0 31.7 %shard_map.46 = bf16[8,128]{1,0:T(8,128)(2,1)} custom-call(bf16[8,128]{1,0:T(8,128)(2,1)} %bitcast.3, s32[64]{0:T(128)} %len_ref.1, bf16[64,4,64,128]{3,2,1,0:T(8,128)(2,1)} %k_ref.1, bf16[64,4,64,128]{3,2,1,0:T(8,128)(2,1)} %v_ref.1), custom_call_target="tpu_custom_call" | custom-call | tf_op jit(solution)/shard_map/pallas_call | solution.py:191
  31.8 1.3 %copy.6 = bf16[1,4,2,128]{3,2,1,0:T(2,128)(2,1)} copy(bf16[1,4,2,128]{3,2,1,0:T(2,128)(2,1)} %bitcast.2) | data formatting | bytes 4096

commit v2 on v1

--- a/solution.py
+++ b/solution.py
@@ -17,9 +17,10 @@
 
 
 def kernel(
-    q_ref, len_ref, k_ref, v_ref, o_ref,
+    q_hbm, len_hbm, k_ref, v_ref, o_ref,
+    q_ref, len_ref,
     kbuf, vbuf, qbuf, r1s, r1r, r2s, r2r,
-    ksem, vsem, q1s_sem, q1r_sem, q2s_sem, q2r_sem, r1s_sem, r1r_sem, r2s_sem, r2r_sem,
+    qsem, lsem, ksem, vsem, q1s_sem, q1r_sem, q2s_sem, q2r_sem, r1s_sem, r1r_sem, r2s_sem, r2r_sem,
 ):
     me = lax.axis_index("ctx")
     z, w = me // NW, me % NW
@@ -42,6 +43,10 @@
                     barrier, inc=1, device_id={"ctx": z * NW + w_at(dx, dc)}, device_id_type=MESH
                 )
 
+    q_load = pltpu.make_async_copy(q_hbm, q_ref, qsem)
+    len_load = pltpu.make_async_copy(len_hbm, len_ref, lsem)
+    q_load.start()
+    len_load.start()
     loads = []
     for i in range(NZ):
         rows = pl.ds(i * NW, NW)
@@ -51,6 +56,8 @@
         loads.append(pltpu.make_async_copy(v_ref.at[rows], vbuf.at[rows], vsem.at[i]))
     for load in loads:
         load.start()
+    q_load.wait()
+    len_load.wait()
     qbuf[w, z] = q_ref[...]
 
     pl.semaphore_wait(barrier, NZ - 1 + NW - 1)
@@ -190,15 +197,17 @@
     vmem, dma = pltpu.VMEM, pltpu.SemaphoreType.DMA
     out = pl.pallas_call(
         kernel,
-        out_shape=jax.ShapeDtypeStruct((8, HEAD_SIZE), BF16),
+        out_shape=pltpu.VMEM((8, HEAD_SIZE), BF16),
         in_specs=[
-            pl.BlockSpec(memory_space=pltpu.VMEM),
-            pl.BlockSpec(memory_space=pltpu.SMEM),
+            pl.BlockSpec(memory_space=pl.ANY),
+            pl.BlockSpec(memory_space=pl.ANY),
             pl.BlockSpec(memory_space=pl.ANY),
             pl.BlockSpec(memory_space=pl.ANY),
         ],
         out_specs=pl.BlockSpec(memory_space=pltpu.VMEM),
         scratch_shapes=[
+            vmem((8, HEAD_SIZE), BF16),
+            pltpu.SMEM((64,), jnp.int32),
             vmem(past_keys.shape, BF16),
             vmem(past_values.shape, BF16),
             vmem((NW, NZ, 8, HEAD_SIZE), BF16),
@@ -206,7 +215,7 @@
             vmem((NW, NZ + 1, 8, HEAD_SIZE), F32),
             vmem((NZ, 2, 8, HEAD_SIZE), F32),
             vmem((NZ, 2, 8, HEAD_SIZE), F32),
-            dma((NZ,)), dma((NZ,)),
+            dma, dma, dma((NZ,)), dma((NZ,)),
             dma((NZ,)), dma((NZ,)), dma((NW,)), dma((NW,)),
             dma((NW,)), dma((NW,)), dma((NZ,)), dma((NZ,)),
         ],

time: 33.2 us -> 30.8 us (0.928)
  Pallas kernels: 31.7 us -> 30.1 us
  local copies, waits for them, and re-layouts: 1.26 us -> 0.58 us
    pallas_call x1, Pallas kernels: 31.7 us -> 30.1 us  [body(): pl.pallas_call(kernel, out_shape=pltpu.VMEM((8, HEAD_SIZE), BF16), in_spe...]
    unnamed x1, local copies, waits for them, and re-layouts: 1.26 us -> 0.58 us
where the time goes in v2:
time: 30.8 us; the launch traced here: 30.7 us
  Pallas kernels  30.1 us (98%)
  local copies, waits for them, and re-layouts  0.58 us (2%)
    pallas_call x1, Pallas kernels, body(): pl.pallas_call(kernel, out_shape=pltpu.VMEM((8, HEAD_SIZE), BF16), in_spe...  30.1 us

profile of v2, /device:TPU:1, one launch (start us, length us, event | category | flops | bytes accessed | tf_op | source)
XLA Modules:
  0.0 30.7 jit_solution(7767651889036139839)
XLA Ops:
  0.0 30.1 %shard_map.46 = bf16[8,128]{1,0:T(8,128)(2,1)S(1)} custom-call(bf16[8,128]{1,0:T(8,128)(2,1)} %bitcast.3, s32[64]{0:T(128)} %len_hbm.1, bf16[64,4,64,128]{3,2,1,0:T(8,128)(2,1)} %k_ref.1, bf16[64,4,64,128]{3,2,1,0:T(8,128)(2,1)} %v_ref.1), custom_call_target="tpu_custom_call" | custom-call | tf_op jit(solution)/shard_map/pallas_call | solution.py:198
  30.1 0.6 %copy.6 = bf16[1,4,2,128]{3,2,1,0:T(2,128)(2,1)} copy(bf16[1,4,2,128]{3,2,1,0:T(2,128)(2,1)S(1)} %bitcast.2) | data formatting | bytes 4096

commit v3 on v2

v3 whole, which is shorter than its diff:
```python
import functools

import jax
import jax.numpy as jnp
from jax import lax
from jax.experimental import pallas as pl
from jax.experimental.pallas import tpu as pltpu
from jax.sharding import PartitionSpec as P

HEAD_SIZE = 128
SCALE = HEAD_SIZE ** (-0.5)
NZ, NX, NC = 8, 4, 2
NW = NX * NC
NEG = -1e30
MESH = pl.DeviceIdType.MESH
F32, BF16 = jnp.float32, jnp.bfloat16


def kernel(
    q_hbm, len_hbm, k_ref, v_ref, o_ref,
    len_ref, kbuf, vbuf, qbuf, r1s, r1r, r2s, r2r,
    qsem, lsem, ksem, vsem, ready,
    xs_sem, xr_sem, zs_sem, zr_sem, r1s_sem, r1r_sem, r2s_sem, r2r_sem,
):
    me = lax.axis_index("ctx")
    z, w = me // NW, me % NW
    x, core = w // NC, w % NC
    late = z // 4
    pair = z // 2

    def w_at(dx, dc):
        return lax.rem(x + dx, NX) * NC + lax.rem(core + dc, NC)

    far_w = [w_at(*d) for d in ((2, 0), (2, 1), (1, 0), (3, 0), (1, 1), (3, 1), (0, 1))]
    pairs = [pair, pair + 1 - 2 * (pair % 2), 3 - pair, (pair + 2) % 4]
    planes = [2 * p + (z + a) % 2 for p in pairs for a in range(2)]
    work = [planes[i] + late * (planes[(i + 4) % NZ] - planes[i]) for i in range(NZ)]
    starts = [work[i] // 2 * 2 for i in range(0, NZ, 2)]

    barrier = pltpu.get_barrier_semaphore()

    def signal(sem, zz, ww):
        pl.semaphore_signal(sem, inc=1, device_id={"ctx": zz * NW + ww}, device_id_type=MESH)

    for ww in far_w:
        signal(barrier, z, ww)
    for zz in planes[1:4]:
        signal(barrier, zz, w)

    @pl.when(late == 0)
    def _():
        for zz in planes[4:]:
            signal(barrier, zz, w)

    q_load = pltpu.make_async_copy(q_hbm, qbuf.at[z, w], qsem)
    len_load = pltpu.make_async_copy(len_hbm, len_ref, lsem)
    q_load.start()
    len_load.start()
    loads = []
    for src, dst, sem in ((k_ref, kbuf, ksem), (v_ref, vbuf, vsem)):
        for i, start in enumerate(starts):
            rows = pl.ds(start * NW, 2 * NW)
            loads.append(pltpu.make_async_copy(src.at[rows], dst.at[rows], sem.at[i]))
    q_load.wait()
    for load in loads:
        load.start()
    pl.semaphore_wait(barrier, 10 + 4 * late)

    @pl.when(late == 1)
    def _():
        for zz in planes[4:]:
            signal(ready.at[z - 4], zz, w)

    def send(src, dst, s_sem, r_sem, zz, ww):
        copy = pltpu.make_async_remote_copy(
            src_ref=src, dst_ref=dst, send_sem=s_sem, recv_sem=r_sem,
            device_id={"ctx": zz * NW + ww}, device_id_type=MESH,
        )
        copy.start()

    def arrived(ref, sem):
        pltpu.make_async_copy(ref, ref, sem).wait()

    for ww in far_w:
        send(qbuf.at[z, w], qbuf.at[z, w], xs_sem, xr_sem, z, ww)
    arrived(qbuf.at[z, pl.ds(0, NW - 1)], xr_sem)
    for i, zz in enumerate(planes):
        if i >= 4:

            @pl.when(late == 0)
            def _():
                pl.semaphore_wait(ready.at[zz - 4], 1)

        if i:
            send(qbuf.at[z], qbuf.at[z], zs_sem, zr_sem.at[z], zz, w)

    base = me * 64
    lane = lax.broadcasted_iota(jnp.int32, (64, 128), 1)
    row = lax.broadcasted_iota(jnp.int32, (128, 128), 0)
    row_head = (row // 2) % 4
    lane8 = lax.broadcasted_iota(jnp.int32, (8, 128), 1)
    lane_t = lane8 % 64 + base
    row2 = lax.broadcasted_iota(jnp.int32, (8, 256), 0)
    lane2 = lax.broadcasted_iota(jnp.int32, (8, 256), 1)
    own_head = (row2 // 2) == (lane2 // 64)

    def attend(step):
        half, first = step // 2, 2 * (step % 2)
        mine = work[2 * step : 2 * step + 2]
        for i in range(2 * step, 2 * step + 2):
            if i % 4:
                arrived(qbuf.at[work[i]], zr_sem.at[work[i]])
            else:

                @pl.when(work[i] != z)
                def _():
                    arrived(qbuf.at[work[i]], zr_sem.at[work[i]])

        loads[step].wait()
        queries = jnp.concatenate(
            [qbuf[zz].astype(F32).reshape(64, 128) for zz in mine], axis=0
        )
        weights = jnp.concatenate(
            [jnp.where(row_head == k, queries, 0.0).astype(BF16) for k in range(4)], axis=1
        )
        members = [(a, ww) for a in range(2) for ww in range(NW)]
        keys = jnp.concatenate(
            [
                jnp.concatenate([kbuf[mine[a] * NW + ww, k] for k in range(4)], axis=1)
                for a, ww in members
            ],
            axis=0,
        )
        wide = lax.dot_general(
            keys, weights, (((1,), (1,)), ((), ())), preferred_element_type=F32
        )
        logit_t = jnp.zeros((64, 128), F32)
        for i in range(len(members)):
            logit_t = jnp.where(lane // 8 == i, wide[i * 64 : (i + 1) * 64], logit_t)
        logit_all = jnp.concatenate([logit_t, logit_t], axis=0).T * SCALE
        loads[4 + step].wait()
        if step == 0:
            len_load.wait()
        for i, (a, ww) in enumerate(members):
            b = mine[a] * NW + ww
            filled = lane_t < len_ref[b]
            logit = jnp.where(filled, logit_all[i * 8 : (i + 1) * 8], NEG)
            top = jnp.max(logit, axis=1, keepdims=True)
            part = jnp.where(filled, jnp.exp(logit - top), 0.0)
            total = jnp.sum(part, axis=1, keepdims=True) * 0.5
            spread = jnp.where(own_head, jnp.concatenate([part, part], axis=1), 0.0)
            high = spread.astype(BF16).astype(F32)
            both = jnp.concatenate([high, spread - high], axis=0).astype(BF16)
            out = jnp.dot(both, vbuf[b].reshape(256, 128), preferred_element_type=F32)
            r1s[half, ww, first + a] = out[:8] + out[8:]
            stats = r1s[half, ww, 4] if first + a else jnp.zeros((8, 128), F32)
            stats = jnp.where(lane8 == first + a, top, stats)
            r1s[half, ww, 4] = jnp.where(lane8 == 4 + first + a, total, stats)

    def reduce(half):
        arrived(r1r.at[half, pl.ds(0, NW - 1)], r1r_sem.at[half])
        st = [r1r[half, s, 4] for s in range(NW)]
        best = functools.reduce(jnp.maximum, st)
        scales = [jnp.exp(t - best) for t in st]
        totals = sum(pltpu.roll(scales[s], 4, 1) * st[s] for s in range(NW))
        for slot in (3, 2, 1, 0):
            zz = work[4 * half + slot]
            acc = jnp.zeros((8, 128), F32)
            for s in range(NW):
                acc += scales[s][:, slot : slot + 1] * r1r[half, s, slot]
            tail = jnp.where(lane8 < 64, best[:, slot : slot + 1], totals[:, 4 + slot : 5 + slot])
            i = 4 * half + slot
            r2s[i, 0] = acc
            r2s[i, 1] = tail
            if slot:
                send(r2s.at[i], r2r.at[z], r2s_sem, r2r_sem, zz, w)
            else:

                @pl.when(zz != z)
                def _():
                    send(r2s.at[i], r2r.at[z], r2s_sem, r2r_sem, zz, w)

                @pl.when(zz == z)
                def _():
                    r2r[z] = r2s[i]


    for half in range(2):
        attend(2 * half)
        attend(2 * half + 1)
        r1r[half, w] = r1s[half, w]
        for ww in far_w:
            send(r1s.at[half, ww], r1r.at[half, w], r1s_sem.at[half], r1r_sem.at[half], z, ww)
    reduce(0)
    reduce(1)
    arrived(r2r.at[pl.ds(0, NZ - 1)], r2r_sem)
    tops = [r2r[s, 1] for s in range(NZ)]
    best = functools.reduce(jnp.maximum, tops)
    acc = jnp.zeros((8, 128), F32)
    total = jnp.zeros((8, 1), F32)
    for s in range(NZ):
        scale = jnp.exp(tops[s][:, :1] - best[:, :1])
        acc += scale * r2r[s, 0]
        total += scale * tops[s][:, 64:65]
    o_ref[...] = (acc / total).astype(o_ref.dtype)
    arrived(qbuf.at[z, pl.ds(0, NW - 1)], xs_sem)
    arrived(qbuf.at[pl.ds(0, NZ - 1)], zs_sem)
    for half in range(2):
        arrived(r1s.at[half, pl.ds(0, NW - 1)], r1s_sem.at[half])
    arrived(r2s.at[pl.ds(0, NZ - 1)], r2s_sem)


def body(query_rows, past_keys, past_values, used_length):
    vmem, dma = pltpu.VMEM, pltpu.SemaphoreType.DMA
    out = pl.pallas_call(
        kernel,
        out_shape=pltpu.VMEM((8, HEAD_SIZE), BF16),
        in_specs=[pl.BlockSpec(memory_space=pl.ANY)] * 4,
        out_specs=pl.BlockSpec(memory_space=pltpu.VMEM),
        scratch_shapes=[
            pltpu.SMEM(used_length.shape, jnp.int32),
            vmem(past_keys.shape, BF16),
            vmem(past_values.shape, BF16),
            vmem((NZ, NW, 8, HEAD_SIZE), BF16),
            vmem((2, NW, 5, 8, HEAD_SIZE), F32),
            vmem((2, NW, 5, 8, HEAD_SIZE), F32),
            vmem((NZ, 2, 8, HEAD_SIZE), F32),
            vmem((NZ, 2, 8, HEAD_SIZE), F32),
            dma, dma, dma((4,)), dma((4,)), pltpu.SemaphoreType.REGULAR((4,)),
            dma, dma, dma, dma((NZ,)), dma((2,)), dma((2,)), dma, dma,
        ],
        compiler_params=pltpu.CompilerParams(collective_id=0, has_side_effects=True),
    )(query_rows.reshape(8, HEAD_SIZE), used_length, past_keys, past_values)
    return out.reshape(query_rows.shape)


def solution(mesh):
    return jax.shard_map(
        body,
        mesh=mesh,
        in_specs=(
            P("ctx", "heads", None, None),
            P(None, "heads", "ctx", None),
            P(None, "heads", "ctx", None),
            P(),
        ),
        out_specs=P("ctx", "heads", None, None),
        check_vma=False,
    )
```

time: 30.8 us -> 27.8 us (0.903)
  Pallas kernels: 30.1 us -> 27.1 us
    pallas_call x1, Pallas kernels: 30.1 us -> 27.1 us  [body(): pl.pallas_call(kernel, out_shape=pltpu.VMEM((8, HEAD_SIZE), BF16), in_spe...]
where the time goes in v3:
time: 27.8 us; the launch traced here: 27.7 us
  Pallas kernels  27.1 us (97%)
  local copies, waits for them, and re-layouts  0.58 us (2%)
    pallas_call x1, Pallas kernels, body(): pl.pallas_call(kernel, out_shape=pltpu.VMEM((8, HEAD_SIZE), BF16), in_spe...  27.1 us
    unnamed x1, local copies, waits for them, and re-layouts  0.58 us

profile of v3, /device:TPU:1, one launch (start us, length us, event | category | flops | bytes accessed | tf_op | source)
XLA Modules:
  0.0 27.7 jit_solution(13437613739005964397)
XLA Ops:
  0.0 27.1 %shard_map.46 = bf16[8,128]{1,0:T(8,128)(2,1)S(1)} custom-call(bf16[8,128]{1,0:T(8,128)(2,1)} %bitcast.3, s32[64]{0:T(128)} %len_hbm.1, bf16[64,4,64,128]{3,2,1,0:T(8,128)(2,1)} %k_ref.1, bf16[64,4,64,128]{3,2,1,0:T(8,128)(2,1)} %v_ref.1), custom_call_target="tpu_custom_call" | custom-call | tf_op jit(solution)/shard_map/pallas_call | solution.py:215
  27.1 0.6 %copy.6 = bf16[1,4,2,128]{3,2,1,0:T(2,128)(2,1)} copy(bf16[1,4,2,128]{3,2,1,0:T(2,128)(2,1)S(1)} %bitcast.2) | data formatting | bytes 4096

commit v4 on v3

--- a/solution.py
+++ b/solution.py
@@ -84,15 +84,20 @@
     for ww in far_w:
         send(qbuf.at[z, w], qbuf.at[z, w], xs_sem, xr_sem, z, ww)
     arrived(qbuf.at[z, pl.ds(0, NW - 1)], xr_sem)
-    for i, zz in enumerate(planes):
+    def send_plane(zz):
+        send(qbuf.at[z], qbuf.at[z], zs_sem, zr_sem.at[z], zz, w)
+
+    for i, zz in enumerate(work):
         if i >= 4:
 
             @pl.when(late == 0)
             def _():
                 pl.semaphore_wait(ready.at[zz - 4], 1)
 
-        if i:
-            send(qbuf.at[z], qbuf.at[z], zs_sem, zr_sem.at[z], zz, w)
+        if i % 4:
+            send_plane(zz)
+        else:
+            pl.when(zz != z)(functools.partial(send_plane, zz))
 
     base = me * 64
     lane = lax.broadcasted_iota(jnp.int32, (64, 128), 1)
@@ -131,8 +136,15 @@
             ],
             axis=0,
         )
-        wide = lax.dot_general(
-            keys, weights, (((1,), (1,)), ((), ())), preferred_element_type=F32
+        wide = jnp.concatenate(
+            [
+                lax.dot_general(
+                    keys[a * 512 : (a + 1) * 512], weights, (((1,), (1,)), ((), ())),
+                    preferred_element_type=F32,
+                )
+                for a in range(2)
+            ],
+            axis=0,
         )
         logit_t = jnp.zeros((64, 128), F32)
         for i in range(len(members)):
@@ -185,12 +197,20 @@
                     r2r[z] = r2s[i]
 
 
+    def share(half, first, count):
+        part = pl.ds(first, count)
+        for ww in far_w:
+            send(
+                r1s.at[half, ww, part], r1r.at[half, w, part],
+                r1s_sem.at[half], r1r_sem.at[half], z, ww,
+            )
+
     for half in range(2):
         attend(2 * half)
+        share(half, 0, 2)
         attend(2 * half + 1)
+        share(half, 2, 3)
         r1r[half, w] = r1s[half, w]
-        for ww in far_w:
-            send(r1s.at[half, ww], r1r.at[half, w], r1s_sem.at[half], r1r_sem.at[half], z, ww)
     reduce(0)
     reduce(1)
     arrived(r2r.at[pl.ds(0, NZ - 1)], r2r_sem)

time: 27.8 us -> 25.7 us (0.924)
  Pallas kernels: 27.1 us -> 25.1 us
    pallas_call x1, Pallas kernels: 27.1 us -> 25.1 us  [body(): pl.pallas_call(kernel, out_shape=pltpu.VMEM((8, HEAD_SIZE), BF16), in_spe...]
where the time goes in v4:
time: 25.7 us; the launch traced here: 25.6 us
  Pallas kernels  25.1 us (98%)
  local copies, waits for them, and re-layouts  0.58 us (2%)
    pallas_call x1, Pallas kernels, body(): pl.pallas_call(kernel, out_shape=pltpu.VMEM((8, HEAD_SIZE), BF16), in_spe...  25.1 us
    unnamed x1, local copies, waits for them, and re-layouts  0.58 us

profile of v4, /device:TPU:1, one launch (start us, length us, event | category | flops | bytes accessed | tf_op | source)
XLA Modules:
  0.0 25.6 jit_solution(1483258628078804550)
XLA Ops:
  0.0 25.1 %shard_map.46 = bf16[8,128]{1,0:T(8,128)(2,1)S(1)} custom-call(bf16[8,128]{1,0:T(8,128)(2,1)} %bitcast.3, s32[64]{0:T(128)} %len_hbm.1, bf16[64,4,64,128]{3,2,1,0:T(8,128)(2,1)} %k_ref.1, bf16[64,4,64,128]{3,2,1,0:T(8,128)(2,1)} %v_ref.1), custom_call_target="tpu_custom_call" | custom-call | tf_op jit(solution)/shard_map/pallas_call | solution.py:235
  25.1 0.6 %copy.6 = bf16[1,4,2,128]{3,2,1,0:T(2,128)(2,1)} copy(bf16[1,4,2,128]{3,2,1,0:T(2,128)(2,1)S(1)} %bitcast.2) | data formatting | bytes 4096

commit v5 on v4

--- a/solution.py
+++ b/solution.py
@@ -20,7 +20,7 @@
     q_hbm, len_hbm, k_ref, v_ref, o_ref,
     len_ref, kbuf, vbuf, qbuf, r1s, r1r, r2s, r2r,
     qsem, lsem, ksem, vsem, ready,
-    xs_sem, xr_sem, zs_sem, zr_sem, r1s_sem, r1r_sem, r2s_sem, r2r_sem,
+    xs_sem, xr_sem, zs_sem, zr_sem, cs_sem, cr_sem, r1s_sem, r1r_sem, r2s_sem, r2r_sem,
 ):
     me = lax.axis_index("ctx")
     z, w = me // NW, me % NW
@@ -81,23 +81,27 @@
     def arrived(ref, sem):
         pltpu.make_async_copy(ref, ref, sem).wait()
 
+    @pl.when(late == 1)
+    def _():
+        for zz in work[:4]:
+            send(qbuf.at[z, w], qbuf.at[z, w], cs_sem, zr_sem.at[z], zz, w)
+
     for ww in far_w:
         send(qbuf.at[z, w], qbuf.at[z, w], xs_sem, xr_sem, z, ww)
     arrived(qbuf.at[z, pl.ds(0, NW - 1)], xr_sem)
-    def send_plane(zz):
+    def send_plane(zz, wait=False):
+        if wait:
+            pl.semaphore_wait(ready.at[zz - 4], 1)
         send(qbuf.at[z], qbuf.at[z], zs_sem, zr_sem.at[z], zz, w)
 
-    for i, zz in enumerate(work):
-        if i >= 4:
-
-            @pl.when(late == 0)
-            def _():
-                pl.semaphore_wait(ready.at[zz - 4], 1)
-
-        if i % 4:
-            send_plane(zz)
-        else:
-            pl.when(zz != z)(functools.partial(send_plane, zz))
+    for zz in planes[1:4]:
+        send_plane(zz)
+
+    @pl.when(late == 0)
+    def _():
+        for zz in planes[4:]:
+            send_plane(zz, True)
+
 
     base = me * 64
     lane = lax.broadcasted_iota(jnp.int32, (64, 128), 1)
@@ -112,16 +116,31 @@
     def attend(step):
         half, first = step // 2, 2 * (step % 2)
         mine = work[2 * step : 2 * step + 2]
-        for i in range(2 * step, 2 * step + 2):
-            if i % 4:
-                arrived(qbuf.at[work[i]], zr_sem.at[work[i]])
-            else:
-
-                @pl.when(work[i] != z)
+        def planes_in():
+            for i in range(2 * step, 2 * step + 2):
+                if i % 4:
+                    arrived(qbuf.at[work[i]], zr_sem.at[work[i]])
+                else:
+
+                    @pl.when(work[i] != z)
+                    def _():
+                        arrived(qbuf.at[work[i]], zr_sem.at[work[i]])
+
+        if half:
+            pl.when(late == 1)(planes_in)
+            if step == 2:
+
+                @pl.when(late == 0)
                 def _():
-                    arrived(qbuf.at[work[i]], zr_sem.at[work[i]])
+                    arrived(qbuf.at[pl.ds(0, NZ - 1), pl.ds(0, 4)], cr_sem)
+
+        else:
+            planes_in()
 
         loads[step].wait()
+        loads[4 + step].wait()
+        if step == 0:
+            len_load.wait()
         queries = jnp.concatenate(
             [qbuf[zz].astype(F32).reshape(64, 128) for zz in mine], axis=0
         )
@@ -150,9 +169,6 @@
         for i in range(len(members)):
             logit_t = jnp.where(lane // 8 == i, wide[i * 64 : (i + 1) * 64], logit_t)
         logit_all = jnp.concatenate([logit_t, logit_t], axis=0).T * SCALE
-        loads[4 + step].wait()
-        if step == 0:
-            len_load.wait()
         for i, (a, ww) in enumerate(members):
             b = mine[a] * NW + ww
             filled = lane_t < len_ref[b]
@@ -197,6 +213,14 @@
                     r2r[z] = r2s[i]
 
 
+    @pl.when(late == 0)
+    def _():
+        column = qbuf.at[pl.ds(4, 4), w]
+        for zz in planes[4:]:
+            arrived(qbuf.at[zz, w], zr_sem.at[zz])
+        for ww in far_w:
+            send(column, column, cs_sem, cr_sem, z, ww)
+
     def share(half, first, count):
         part = pl.ds(first, count)
         for ww in far_w:
@@ -205,13 +229,18 @@
                 r1s_sem.at[half], r1r_sem.at[half], z, ww,
             )
 
-    for half in range(2):
-        attend(2 * half)
-        share(half, 0, 2)
-        attend(2 * half + 1)
-        share(half, 2, 3)
-        r1r[half, w] = r1s[half, w]
+    attend(0)
+    share(0, 0, 2)
+    attend(1)
+    share(0, 2, 3)
+    r1r[0, w] = r1s[0, w]
+    attend(2)
+    pl.when(late == 0)(lambda: share(1, 0, 2))
+    attend(3)
+    pl.when(late == 0)(lambda: share(1, 2, 3))
+    r1r[1, w] = r1s[1, w]
     reduce(0)
+    pl.when(late == 1)(lambda: share(1, 0, 5))
     reduce(1)
     arrived(r2r.at[pl.ds(0, NZ - 1)], r2r_sem)
     tops = [r2r[s, 1] for s in range(NZ)]
@@ -224,7 +253,17 @@
         total += scale * tops[s][:, 64:65]
     o_ref[...] = (acc / total).astype(o_ref.dtype)
     arrived(qbuf.at[z, pl.ds(0, NW - 1)], xs_sem)
-    arrived(qbuf.at[pl.ds(0, NZ - 1)], zs_sem)
+
+    @pl.when(late == 0)
+    def _():
+        arrived(qbuf.at[pl.ds(0, NZ - 1)], zs_sem)
+        arrived(qbuf.at[pl.ds(0, NZ - 1), pl.ds(0, 4)], cs_sem)
+
+    @pl.when(late == 1)
+    def _():
+        arrived(qbuf.at[pl.ds(0, 3)], zs_sem)
+        arrived(qbuf.at[0, pl.ds(0, 4)], cs_sem)
+
     for half in range(2):
         arrived(r1s.at[half, pl.ds(0, NW - 1)], r1s_sem.at[half])
     arrived(r2s.at[pl.ds(0, NZ - 1)], r2s_sem)
@@ -247,7 +286,7 @@
             vmem((NZ, 2, 8, HEAD_SIZE), F32),
             vmem((NZ, 2, 8, HEAD_SIZE), F32),
             dma, dma, dma((4,)), dma((4,)), pltpu.SemaphoreType.REGULAR((4,)),
-            dma, dma, dma, dma((NZ,)), dma((2,)), dma((2,)), dma, dma,
+            dma, dma, dma, dma((NZ,)), dma, dma, dma((2,)), dma((2,)), dma, dma,
         ],
         compiler_params=pltpu.CompilerParams(collective_id=0, has_side_effects=True),
     )(query_rows.reshape(8, HEAD_SIZE), used_length, past_keys, past_values)

time: 25.7 us -> 25.5 us (level)
  Pallas kernels: 25.1 us -> 24.8 us
    pallas_call x1, Pallas kernels: 25.1 us -> 24.8 us  [body(): pl.pallas_call(kernel, out_shape=pltpu.VMEM((8, HEAD_SIZE), BF16), in_spe...]
where the time goes in v5:
time: 25.5 us; the launch traced here: 25.4 us
  Pallas kernels  24.8 us (97%)
  local copies, waits for them, and re-layouts  0.58 us (2%)
    pallas_call x1, Pallas kernels, body(): pl.pallas_call(kernel, out_shape=pltpu.VMEM((8, HEAD_SIZE), BF16), in_spe...  24.8 us
    unnamed x1, local copies, waits for them, and re-layouts  0.58 us

profile of v5, /device:TPU:1, one launch (start us, length us, event | category | flops | bytes accessed | tf_op | source)
XLA Modules:
  0.0 25.4 jit_solution(4499639896594844301)
XLA Ops:
  0.0 24.8 %shard_map.46 = bf16[8,128]{1,0:T(8,128)(2,1)S(1)} custom-call(bf16[8,128]{1,0:T(8,128)(2,1)} %bitcast.3, s32[64]{0:T(128)} %len_hbm.1, bf16[64,4,64,128]{3,2,1,0:T(8,128)(2,1)} %k_ref.1, bf16[64,4,64,128]{3,2,1,0:T(8,128)(2,1)} %v_ref.1), custom_call_target="tpu_custom_call" | custom-call | tf_op jit(solution)/shard_map/pallas_call | solution.py:274
  24.8 0.6 %copy.6 = bf16[1,4,2,128]{3,2,1,0:T(2,128)(2,1)} copy(bf16[1,4,2,128]{3,2,1,0:T(2,128)(2,1)S(1)} %bitcast.2) | data formatting | bytes 4096

commit v6 on v5

--- a/solution.py
+++ b/solution.py
@@ -44,13 +44,8 @@
 
     for ww in far_w:
         signal(barrier, z, ww)
-    for zz in planes[1:4]:
-        signal(barrier, zz, w)
-
-    @pl.when(late == 0)
-    def _():
-        for zz in planes[4:]:
-            signal(barrier, zz, w)
+    for zz in range(NZ - 1, 0, -1):
+        pl.when(zz > z)(functools.partial(signal, barrier, zz, w))
 
     q_load = pltpu.make_async_copy(q_hbm, qbuf.at[z, w], qsem)
     len_load = pltpu.make_async_copy(len_hbm, len_ref, lsem)
@@ -64,12 +59,10 @@
     q_load.wait()
     for load in loads:
         load.start()
-    pl.semaphore_wait(barrier, 10 + 4 * late)
-
-    @pl.when(late == 1)
-    def _():
-        for zz in planes[4:]:
-            signal(ready.at[z - 4], zz, w)
+    pl.semaphore_wait(barrier, NW - 1 + z)
+
+    for zz in range(NZ - 1):
+        pl.when(zz < z)(functools.partial(signal, ready.at[z], zz, w))
 
     def send(src, dst, s_sem, r_sem, zz, ww):
         copy = pltpu.make_async_remote_copy(
@@ -89,9 +82,11 @@
     for ww in far_w:
         send(qbuf.at[z, w], qbuf.at[z, w], xs_sem, xr_sem, z, ww)
     arrived(qbuf.at[z, pl.ds(0, NW - 1)], xr_sem)
-    def send_plane(zz, wait=False):
-        if wait:
-            pl.semaphore_wait(ready.at[zz - 4], 1)
+    def send_plane(zz):
+        @pl.when(zz > z)
+        def _():
+            pl.semaphore_wait(ready.at[zz], 1)
+
         send(qbuf.at[z], qbuf.at[z], zs_sem, zr_sem.at[z], zz, w)
 
     for zz in planes[1:4]:
@@ -100,7 +95,7 @@
     @pl.when(late == 0)
     def _():
         for zz in planes[4:]:
-            send_plane(zz, True)
+            send_plane(zz)
 
 
     base = me * 64
@@ -285,7 +280,7 @@
             vmem((2, NW, 5, 8, HEAD_SIZE), F32),
             vmem((NZ, 2, 8, HEAD_SIZE), F32),
             vmem((NZ, 2, 8, HEAD_SIZE), F32),
-            dma, dma, dma((4,)), dma((4,)), pltpu.SemaphoreType.REGULAR((4,)),
+            dma, dma, dma((4,)), dma((4,)), pltpu.SemaphoreType.REGULAR((NZ,)),
             dma, dma, dma, dma((NZ,)), dma, dma, dma((2,)), dma((2,)), dma, dma,
         ],
         compiler_params=pltpu.CompilerParams(collective_id=0, has_side_effects=True),

time: 25.5 us -> 25.2 us (0.988)
  no operation moved by 1% of the time
where the time goes in v6:
time: 25.2 us; the launch traced here: 25.1 us
  Pallas kernels  24.6 us (98%)
  local copies, waits for them, and re-layouts  0.58 us (2%)
    pallas_call x1, Pallas kernels, body(): pl.pallas_call(kernel, out_shape=pltpu.VMEM((8, HEAD_SIZE), BF16), in_spe...  24.6 us
    unnamed x1, local copies, waits for them, and re-layouts  0.58 us

profile of v6, /device:TPU:1, one launch (start us, length us, event | category | flops | bytes accessed | tf_op | source)
XLA Modules:
  0.0 25.1 jit_solution(10185143413025735115)
XLA Ops:
  0.0 24.6 %shard_map.46 = bf16[8,128]{1,0:T(8,128)(2,1)S(1)} custom-call(bf16[8,128]{1,0:T(8,128)(2,1)} %bitcast.3, s32[64]{0:T(128)} %len_hbm.1, bf16[64,4,64,128]{3,2,1,0:T(8,128)(2,1)} %k_ref.1, bf16[64,4,64,128]{3,2,1,0:T(8,128)(2,1)} %v_ref.1), custom_call_target="tpu_custom_call" | custom-call | tf_op jit(solution)/shard_map/pallas_call | solution.py:269
  24.6 0.6 %copy.6 = bf16[1,4,2,128]{3,2,1,0:T(2,128)(2,1)} copy(bf16[1,4,2,128]{3,2,1,0:T(2,128)(2,1)S(1)} %bitcast.2) | data formatting | bytes 4096

commit v7 on v5

--- a/solution.py
+++ b/solution.py
@@ -18,9 +18,9 @@
 
 def kernel(
     q_hbm, len_hbm, k_ref, v_ref, o_ref,
-    len_ref, kbuf, vbuf, qbuf, r1s, r1r, r2s, r2r,
+    len_ref, kbuf, vbuf, qbuf, r1s, r1r, r2s, r2r, t2s, t2r,
     qsem, lsem, ksem, vsem, ready,
-    xs_sem, xr_sem, zs_sem, zr_sem, cs_sem, cr_sem, r1s_sem, r1r_sem, r2s_sem, r2r_sem,
+    xs_sem, xr_sem, zs_sem, zr_sem, cs_sem, cr_sem, r1s_sem, r1r_sem, r2s_sem, r2r_sem, t2s_sem, t2r_sem,
 ):
     me = lax.axis_index("ctx")
     z, w = me // NW, me % NW
@@ -191,26 +191,29 @@
         best = functools.reduce(jnp.maximum, st)
         scales = [jnp.exp(t - best) for t in st]
         totals = sum(pltpu.roll(scales[s], 4, 1) * st[s] for s in range(NW))
+        rows = jnp.concatenate([jnp.where(lane8 < 4, best, totals)] * 16, axis=0).T
         for slot in (3, 2, 1, 0):
             zz = work[4 * half + slot]
             acc = jnp.zeros((8, 128), F32)
             for s in range(NW):
                 acc += scales[s][:, slot : slot + 1] * r1r[half, s, slot]
-            tail = jnp.where(lane8 < 64, best[:, slot : slot + 1], totals[:, 4 + slot : 5 + slot])
             i = 4 * half + slot
-            r2s[i, 0] = acc
-            r2s[i, 1] = tail
+            r2s[i] = acc
+            t2s[i] = jnp.where(lane8[:1] < 64, rows[slot : slot + 1], rows[4 + slot : 5 + slot])
+
+            def send_sum(i=i, zz=zz):
+                send(r2s.at[i], r2r.at[z], r2s_sem, r2r_sem, zz, w)
+                send(t2s.at[i], t2r.at[z], t2s_sem, t2r_sem, zz, w)
+
             if slot:
-                send(r2s.at[i], r2r.at[z], r2s_sem, r2r_sem, zz, w)
+                send_sum()
             else:
-
-                @pl.when(zz != z)
-                def _():
-                    send(r2s.at[i], r2r.at[z], r2s_sem, r2r_sem, zz, w)
+                pl.when(zz != z)(send_sum)
 
                 @pl.when(zz == z)
                 def _():
                     r2r[z] = r2s[i]
+                    t2r[z] = t2s[i]
 
 
     @pl.when(late == 0)
@@ -242,16 +245,17 @@
     reduce(0)
     pl.when(late == 1)(lambda: share(1, 0, 5))
     reduce(1)
+    arrived(t2r.at[pl.ds(0, NZ - 1)], t2r_sem)
     arrived(r2r.at[pl.ds(0, NZ - 1)], r2r_sem)
-    tops = [r2r[s, 1] for s in range(NZ)]
-    best = functools.reduce(jnp.maximum, tops)
+    tails = t2r[...].reshape(NZ, HEAD_SIZE)
+    scales = jnp.exp(tails - jnp.max(tails, axis=0, keepdims=True))
+    totals = jnp.sum(pltpu.roll(scales, 64, 1) * tails, axis=0, keepdims=True)
+    scales = scales / pltpu.roll(jnp.broadcast_to(totals, (NZ, HEAD_SIZE)), 64, 1)
+    scales = jnp.concatenate([scales] * 16, axis=0).T[:8]
     acc = jnp.zeros((8, 128), F32)
-    total = jnp.zeros((8, 1), F32)
     for s in range(NZ):
-        scale = jnp.exp(tops[s][:, :1] - best[:, :1])
-        acc += scale * r2r[s, 0]
-        total += scale * tops[s][:, 64:65]
-    o_ref[...] = (acc / total).astype(o_ref.dtype)
+        acc += scales[:, s : s + 1] * r2r[s]
+    o_ref[...] = acc.astype(o_ref.dtype)
     arrived(qbuf.at[z, pl.ds(0, NW - 1)], xs_sem)
 
     @pl.when(late == 0)
@@ -267,6 +271,7 @@
     for half in range(2):
         arrived(r1s.at[half, pl.ds(0, NW - 1)], r1s_sem.at[half])
     arrived(r2s.at[pl.ds(0, NZ - 1)], r2s_sem)
+    arrived(t2s.at[pl.ds(0, NZ - 1)], t2s_sem)
 
 
 def body(query_rows, past_keys, past_values, used_length):
@@ -283,10 +288,12 @@
             vmem((NZ, NW, 8, HEAD_SIZE), BF16),
             vmem((2, NW, 5, 8, HEAD_SIZE), F32),
             vmem((2, NW, 5, 8, HEAD_SIZE), F32),
-            vmem((NZ, 2, 8, HEAD_SIZE), F32),
-            vmem((NZ, 2, 8, HEAD_SIZE), F32),
+            vmem((NZ, 8, HEAD_SIZE), F32),
+            vmem((NZ, 8, HEAD_SIZE), F32),
+            vmem((NZ, 1, HEAD_SIZE), F32),
+            vmem((NZ, 1, HEAD_SIZE), F32),
             dma, dma, dma((4,)), dma((4,)), pltpu.SemaphoreType.REGULAR((4,)),
-            dma, dma, dma, dma((NZ,)), dma, dma, dma((2,)), dma((2,)), dma, dma,
+            dma, dma, dma, dma((NZ,)), dma, dma, dma((2,)), dma((2,)), dma, dma, dma, dma,
         ],
         compiler_params=pltpu.CompilerParams(collective_id=0, has_side_effects=True),
     )(query_rows.reshape(8, HEAD_SIZE), used_length, past_keys, past_values)

time: 25.5 us -> 25.6 us (level)
  no operation moved by 1% of the time
where the time goes in v7:
time: 25.6 us; the launch traced here: 25.5 us
  Pallas kernels  24.9 us (97%)
  local copies, waits for them, and re-layouts  0.58 us (2%)
    pallas_call x1, Pallas kernels, body(): pl.pallas_call(kernel, out_shape=pltpu.VMEM((8, HEAD_SIZE), BF16), in_spe...  24.9 us
    unnamed x1, local copies, waits for them, and re-layouts  0.58 us

profile of v7, /device:TPU:1, one launch (start us, length us, event | category | flops | bytes accessed | tf_op | source)
XLA Modules:
  0.0 25.5 jit_solution(14928919829241568893)
XLA Ops:
  0.0 24.9 %shard_map.46 = bf16[8,128]{1,0:T(8,128)(2,1)S(1)} custom-call(bf16[8,128]{1,0:T(8,128)(2,1)} %bitcast.3, s32[64]{0:T(128)} %len_hbm.1, bf16[64,4,64,128]{3,2,1,0:T(8,128)(2,1)} %k_ref.1, bf16[64,4,64,128]{3,2,1,0:T(8,128)(2,1)} %v_ref.1), custom_call_target="tpu_custom_call" | custom-call | tf_op jit(solution)/shard_map/pallas_call | solution.py:279
  24.9 0.6 %copy.6 = bf16[1,4,2,128]{3,2,1,0:T(2,128)(2,1)} copy(bf16[1,4,2,128]{3,2,1,0:T(2,128)(2,1)S(1)} %bitcast.2) | data formatting | bytes 4096
